TPU v7x, 32 devices: a whole 2x2x4 slice. The times are simulated.
32 devices in a mesh: samples: 4 (over y, x), features: 4 (over z), rhs: 2 (over core).
Axes of the slice: x: 2, y: 2, z: 4, core: 2. Of those that a mesh axis runs over, the one named last changes fastest.
Arguments:
- design: bfloat16 [32768, 32768], P(('samples', 'rhs'), 'features'), may hold values from -0.03125 to 0.03125
- right_side: float32 [32768, 64], P('features', 'rhs'), may hold values from -6 to 6
- factor: bfloat16 [32768, 768], P('features', 'rhs'), may hold values from -0.03125 to 0.03125
- nystrom_values: float32 [768], replicated, may hold values from 0.5 to 3
Outputs:
- solution: float32 [32768, 64], P('features', 'rhs')
- residual: float32 [32768, 64], P('features', 'rhs')
All inputs are finite; a program needn't handle non-finite values.
Results may differ from a plain program's by a relative error of at most 0.0181.
Values may be sent and summed in bfloat16 or wider, within the bound.
A program may use at most 192 MiB of HBM per device.

v0:
```python
import jax
import jax.numpy as jnp
from jax import lax
from jax.sharding import PartitionSpec as P

ITERS = 3


ridge_weight = 1.0


def inner_prod(left, right):
    return lax.dot_general(
        left,
        right,
        (((0,), (0,)), ((), ())),
        precision=lax.Precision.HIGHEST,
        preferred_element_type=jnp.float32,
    )


def split_parts(values):
    upper = values.astype(jnp.bfloat16)
    widened = lax.optimization_barrier(upper).astype(jnp.float32)
    lower = (values - widened).astype(jnp.bfloat16)
    return (upper, lower)


def factor_inner(factor_narrow, values):
    upper, lower = split_parts(values)
    dims = (((0,), (0,)), ((), ()))
    first = lax.dot_general(factor_narrow, upper, dims, preferred_element_type=jnp.float32)
    second = lax.dot_general(factor_narrow, lower, dims, preferred_element_type=jnp.float32)
    return first + second


def factor_times(factor_narrow, values):
    upper, lower = split_parts(values)
    first = jnp.dot(factor_narrow, upper, preferred_element_type=jnp.float32)
    second = jnp.dot(factor_narrow, lower, preferred_element_type=jnp.float32)
    return first + second


def shards(design, right_side, factor, nystrom_values):
    feat_rows, col_share = right_side.shape
    shrink = (1.0 + jnp.min(nystrom_values)) / (1.0 + nystrom_values) - 1.0
    columns = lax.all_gather(right_side, "rhs", axis=1, tiled=True)
    residual = columns
    basis_rows = lax.all_gather(factor, "rhs", axis=1, tiled=True)

    def totals(values):
        return lax.psum(values, "features")

    def expand(projected):
        return factor_times(basis_rows, shrink[:, None] * projected)

    projected = totals(factor_inner(basis_rows, residual))
    direction = residual + expand(projected)
    solution = jnp.zeros_like(residual)
    for iteration in range(ITERS):
        narrow = direction.astype(jnp.bfloat16)
        apply_partial_value = jnp.dot(design, narrow, preferred_element_type=jnp.float32)
        narrow_images = lax.psum(apply_partial_value, "features").astype(jnp.bfloat16)
        feature_term = lax.dot_general(
            design, narrow_images, (((0,), (0,)), ((), ())), preferred_element_type=jnp.float32
        )
        summed = lax.psum(feature_term, ("samples", "rhs"))
        applied = summed + ridge_weight * direction
        gram_block, cross_term, image_res, image_image, factor_image = totals(
            (
                inner_prod(direction, applied),
                inner_prod(direction, residual),
                inner_prod(applied, residual),
                inner_prod(applied, applied),
                factor_inner(basis_rows, applied),
            )
        )
        gram_block = 0.5 * (gram_block + gram_block.T)
        chol_lower = jnp.linalg.cholesky(gram_block)
        unit_dir = jax.scipy.linalg.solve_triangular(chol_lower, direction.T, lower=True).T
        unit_img = jax.scipy.linalg.solve_triangular(chol_lower, applied.T, lower=True).T
        step_coef = jax.scipy.linalg.solve_triangular(chol_lower, cross_term, lower=True)
        solution = solution + jnp.dot(unit_dir, step_coef, precision=lax.Precision.HIGHEST)
        residual = residual - jnp.dot(unit_img, step_coef, precision=lax.Precision.HIGHEST)
        if iteration + 1 < ITERS:
            back_step = jax.scipy.linalg.solve_triangular(
                chol_lower, step_coef, lower=True, trans=1
            )
            projected = projected - jnp.dot(
                factor_image, back_step, precision=lax.Precision.HIGHEST
            )
            scaled = residual + expand(projected)
            image_new = image_res - jnp.dot(image_image, back_step, precision=lax.Precision.HIGHEST)
            image_new = image_new + inner_prod(factor_image, shrink[:, None] * projected)
            next_coef = -jax.scipy.linalg.solve_triangular(chol_lower, image_new, lower=True)
            direction = scaled + jnp.dot(unit_dir, next_coef, precision=lax.Precision.HIGHEST)
    column_start = lax.axis_index("rhs") * col_share
    out_sol = lax.dynamic_slice_in_dim(solution, column_start, col_share, 1)
    out_res = lax.dynamic_slice_in_dim(residual, column_start, col_share, 1)
    return (out_sol, out_res)


def solution(mesh):
    placed = (P(("samples", "rhs"), "features"), P("features", "rhs"), P("features", "rhs"), P())
    return jax.shard_map(
        shards,
        mesh=mesh,
        in_specs=placed,
        out_specs=(P("features", "rhs"), P("features", "rhs")),
        check_vma=False,
    )
```

profile of v0, /device:TPU:0, one launch (start us, length us, event | category | flops | bytes accessed | tf_op | source)
XLA Modules:
  0.0 853.2 jit_solution(9998928612973178029)
XLA Ops:
  10.0 12.9 %all-gather.3.cloned.1.call-done = f32[8192,64]{0,1:T(8,128)} async-done(((f32[8192,32]{0,1:T(8,128)}), f32[8192,64]{0,1:T(8,128)}) %all-gather.3.cloned.1.call-update) | async-done | bytes 2097168 | tf_op jit(solution)/shard_map/all_gather | solution.py:47
  24.7 25.6 %all-gather.5.cloned.1.call-done = bf16[8192,768]{1,0:T(8,128)(2,1)} async-done(((bf16[8192,384]{1,0:T(8,128)(2,1)}), bf16[8192,768]{1,0:T(8,128)(2,1)}) %all-gather.5.cloned.1.call-update) | async-done | bytes 12582928 | tf_op jit(solution)/shard_map/all_gather | solution.py:49
  61.5 36.2 %all-reduce.15.cloned.1.call-done = f32[768,64]{0,1:T(8,128)} async-done(((f32[768,64]{0,1:T(8,128)}), f32[768,64]{0,1:T(8,128)}) %all-reduce.15.cloned.1.call-update) | async-done | bytes 196624 | tf_op jit(solution)/shard_map/psum | solution.py:52
  98.7 8.5 fusion.67
  107.2 9.8 %fusion.3 = f32[8192,64]{0,1:T(8,128)} fusion(f32[8192,64]{0,1:T(8,128)S(1)} %copy-done.1, f32[64,8192]{1,0:T(8,128)S(1)} %fusion.67, bf16[8192,768]{1,0:T(8,128)(2,1)} %all-gather.5.cloned.1.call-done, bf16[768,64]{0,1:T(8,128)(2,1)S(1)} %multiply_convert_fusion, f32[768,64]{0,1:T(8,128)S(1)} %copy-done.19, f32[768]{0:T(1024)S(1)} %divide_add_fusion), kind=kOutput, calls=%fused_computation.13 | convolution fusion | flops 806551552 | bytes 19172352 | tf_op jit(solution)/shard_map/dot_general | solution.py:40
  117.1 30.4 %convolution_bitcast_fusion.5 = f32[4096,64]{0,1:T(8,128)S(1)} fusion(bf16[4096,8192]{1,0:T(8,128)(2,1)} %param.11, f32[8192,64]{0,1:T(8,128)} %fusion.3), kind=kOutput, calls=%fused_computation.18 | convolution fusion | flops 4295491584 | bytes 70254592 | tf_op jit(solution)/shard_map/dot_general | solution.py:62
  147.4 42.8 %all-reduce.30 = bf16[4096,64]{0,1:T(8,128)(2,1)} all-reduce(f32[4096,64]{0,1:T(8,128)S(1)} %convolution_bitcast_fusion.5), channel_id=1, replica_groups=mesh['samples'=4,'features'=4,'rhs'=2] {'features'}, use_global_device_ids=true, to_apply=%region_2.0 | all-reduce | flops 262144 | bytes 1572864 | tf_op jit(solution)/shard_map/psum | solution.py:63
  190.2 25.9 %convolution_bitcast_fusion.2 = f32[8192,64]{0,1:T(8,128)} fusion(bf16[4096,8192]{1,0:T(8,128)(2,1)} %param.11, bf16[4096,64]{0,1:T(8,128)(2,1)} %all-reduce.30), kind=kOutput, calls=%fused_computation.10 | convolution fusion | flops 4294967296 | bytes 69730304 | tf_op jit(solution)/shard_map/dot_general | solution.py:64
  220.2 57.3 %all-reduce.17.cloned.1.call-done = f32[8192,64]{0,1:T(8,128)} async-done(((f32[8192,64]{0,1:T(8,128)}), f32[8192,64]{0,1:T(8,128)}) %all-reduce.17.cloned.1.call-update) | async-done | bytes 2097168 | tf_op jit(solution)/shard_map/psum | solution.py:67
  302.0 19.4 %all-reduce.29.cloned.1.call-done = (f32[64,64]{1,0:T(8,128)}, f32[64,64]{1,0:T(8,128)}, f32[64,64]{1,0:T(8,128)}, f32[64,64]{1,0:T(8,128)}) async-done(((f32[64,64]{1,0:T(8,128)}, f32[64,64]{1,0:T(8,128)}, f32[64,64]{1,0:T(8,128)}, f32[64,64]{1,0:T(8,128)}), (f32[64,64]{1,0:T(8,128)}, f32[64,64]{1,0:T(8,128)}, f32[64,64]{1,0:T(8,128)}, f32[64,64]{1,0:T(8,128)})) %all-reduce.29.cloned.1.call-update) | async-done | bytes 65552 | tf_op jit(solution)/shard_map/psum | solution.py:52
  344.5 14.6 %all-reduce.19.cloned.1.call-done = f32[768,64]{0,1:T(8,128)} async-done(((f32[768,64]{0,1:T(8,128)}), f32[768,64]{0,1:T(8,128)}) %all-reduce.19.cloned.1.call-update) | async-done | bytes 196624 | tf_op jit(solution)/shard_map/psum | solution.py:52
  370.6 8.6 %fusion.4 = f32[8192,64]{0,1:T(8,128)S(1)} fusion(f32[8192,64]{0,1:T(8,128)S(1)} %convolution_subtract_fusion.1, f32[64,8192]{1,0:T(8,128)S(1)} %fusion.72, bf16[8192,768]{1,0:T(8,128)(2,1)} %all-gather.5.cloned.1.call-done, bf16[768,64]{0,1:T(8,128)(2,1)S(1)} %get-tuple-element.20, f32[768,64]{0,1:T(8,128)S(1)} %get-tuple-element.21, ...), kind=kOutput, calls=%fused_computation.14 | convolution fusion | flops 806551552 | bytes 19172352 | tf_op jit(solution)/shard_map/dot_general | solution.py:40
  381.5 27.8 %convolution_bitcast_fusion.4 = f32[4096,64]{0,1:T(8,128)S(1)} fusion(bf16[4096,8192]{1,0:T(8,128)(2,1)} %param.11, f32[8192,64]{0,1:T(8,128)S(1)} %convolution_add_fusion.2), kind=kOutput, calls=%fused_computation.17 | convolution fusion | flops 4295491584 | bytes 70254592 | tf_op jit(solution)/shard_map/dot_general | solution.py:62
  409.4 42.1 %all-reduce.31 = bf16[4096,64]{0,1:T(8,128)(2,1)} all-reduce(f32[4096,64]{0,1:T(8,128)S(1)} %convolution_bitcast_fusion.4), channel_id=1, replica_groups=mesh['samples'=4,'features'=4,'rhs'=2] {'features'}, use_global_device_ids=true, to_apply=%region_11.0 | all-reduce | flops 262144 | bytes 1572864 | tf_op jit(solution)/shard_map/psum | solution.py:63
  451.5 25.9 %convolution_bitcast_fusion.1 = f32[8192,64]{0,1:T(8,128)} fusion(bf16[4096,8192]{1,0:T(8,128)(2,1)} %param.11, bf16[4096,64]{0,1:T(8,128)(2,1)} %all-reduce.31), kind=kOutput, calls=%fused_computation.5 | convolution fusion | flops 4294967296 | bytes 69730304 | tf_op jit(solution)/shard_map/dot_general | solution.py:64
  481.9 57.4 %all-reduce.21.cloned.1.call-done = f32[8192,64]{0,1:T(8,128)} async-done(((f32[8192,64]{0,1:T(8,128)}), f32[8192,64]{0,1:T(8,128)}) %all-reduce.21.cloned.1.call-update) | async-done | bytes 2097168 | tf_op jit(solution)/shard_map/psum | solution.py:67
  564.2 19.4 %all-reduce.27.cloned.1.call-done = (f32[64,64]{1,0:T(8,128)}, f32[64,64]{1,0:T(8,128)}, f32[64,64]{1,0:T(8,128)}, f32[64,64]{1,0:T(8,128)}) async-done(((f32[64,64]{1,0:T(8,128)}, f32[64,64]{1,0:T(8,128)}, f32[64,64]{1,0:T(8,128)}, f32[64,64]{1,0:T(8,128)}), (f32[64,64]{1,0:T(8,128)}, f32[64,64]{1,0:T(8,128)}, f32[64,64]{1,0:T(8,128)}, f32[64,64]{1,0:T(8,128)})) %all-reduce.27.cloned.1.call-update) | async-done | bytes 65552 | tf_op jit(solution)/shard_map/psum | solution.py:52
  606.6 14.8 %all-reduce.23.cloned.1.call-done = f32[768,64]{0,1:T(8,128)} async-done(((f32[768,64]{0,1:T(8,128)}), f32[768,64]{0,1:T(8,128)}) %all-reduce.23.cloned.1.call-update) | async-done | bytes 196624 | tf_op jit(solution)/shard_map/psum | solution.py:52
  632.9 8.6 %fusion.5 = f32[8192,64]{0,1:T(8,128)S(1)} fusion(f32[8192,64]{0,1:T(8,128)S(1)} %convolution_subtract_fusion, f32[64,8192]{1,0:T(8,128)S(1)} %fusion.79, bf16[8192,768]{1,0:T(8,128)(2,1)} %all-gather.5.cloned.1.call-done, f32[768,64]{0,1:T(8,128)S(1)} %get-tuple-element.23, bf16[768,64]{0,1:T(8,128)(2,1)S(1)} %get-tuple-element.22), kind=kOutput, calls=%fused_computation.15 | convolution fusion | flops 806502400 | bytes 19169280 | tf_op jit(solution)/shard_map/dot_general | solution.py:40
  644.0 27.1 %convolution_bitcast_fusion.3 = f32[4096,64]{0,1:T(8,128)S(1)} fusion(bf16[4096,8192]{1,0:T(8,128)(2,1)} %param.11, f32[8192,64]{0,1:T(8,128)S(1)} %convolution_add_fusion), kind=kOutput, calls=%fused_computation.16 | convolution fusion | flops 4295491584 | bytes 70254592 | tf_op jit(solution)/shard_map/dot_general | solution.py:62
  671.1 42.1 %all-reduce.32 = bf16[4096,64]{0,1:T(8,128)(2,1)} all-reduce(f32[4096,64]{0,1:T(8,128)S(1)} %convolution_bitcast_fusion.3), channel_id=1, replica_groups=mesh['samples'=4,'features'=4,'rhs'=2] {'features'}, use_global_device_ids=true, to_apply=%region_18.0 | all-reduce | flops 262144 | bytes 1572864 | tf_op jit(solution)/shard_map/psum | solution.py:63
  713.2 25.9 %convolution_bitcast_fusion = f32[8192,64]{0,1:T(8,128)} fusion(bf16[4096,8192]{1,0:T(8,128)(2,1)} %param.11, bf16[4096,64]{0,1:T(8,128)(2,1)} %all-reduce.32), kind=kOutput, calls=%fused_computation | convolution fusion | flops 4294967296 | bytes 69730304 | tf_op jit(solution)/shard_map/dot_general | solution.py:64
  750.0 50.6 %all-reduce.25.cloned.1.call-done = f32[8192,64]{0,1:T(8,128)} async-done(((f32[8192,64]{0,1:T(8,128)}), f32[8192,64]{0,1:T(8,128)}) %all-reduce.25.cloned.1.call-update) | async-done | bytes 2097168 | tf_op jit(solution)/shard_map/psum | solution.py:67
  804.1 19.8 %all-reduce = (f32[64,64]{1,0:T(8,128)S(1)}, f32[64,64]{1,0:T(8,128)S(1)}) all-reduce(f32[64,64]{1,0:T(8,128)S(1)} %fusion.19, f32[64,64]{1,0:T(8,128)S(1)} %fusion.83), channel_id=1, replica_groups=mesh['samples'=4,'features'=4,'rhs'=2] {'features'}, use_global_device_ids=true, to_apply=%region_20.25 | all-reduce | flops 8192 | bytes 65536 | tf_op jit(solution)/shard_map/psum | solution.py:52
  (157 shorter events, 183.9 us)
Async XLA Ops:
  7.2 15.7 %all-gather.3.cloned.1.call-start = ((), (), s32[]{:S(2)}) async-start(), calls=%async_computation | async-start | bytes 3145728 | tf_op jit(solution)/shard_map/all_gather | solution.py:47
  7.9 42.4 %all-gather.5.cloned.1.call-start = ((), (), s32[]{:S(2)}) async-start(), calls=%async_computation.1 | async-start | bytes 18874368 | tf_op jit(solution)/shard_map/all_gather | solution.py:49
  8.7 89.1 %all-reduce.15.cloned.1.call-start = ((), (), s32[]{:S(2)}) async-start(), calls=%async_computation.2 | async-start | bytes 393216 | tf_op jit(solution)/shard_map/psum | solution.py:52
  22.8 27.4 %copy-start.1 = (f32[8192,64]{0,1:T(8,128)S(1)}, f32[8192,64]{0,1:T(8,128)}, u32[]{:S(2)}) copy-start(f32[8192,64]{0,1:T(8,128)} %all-gather.3.cloned.1.call-done) | copy-start | bytes 6291460
  50.3 8.2 copy-start
  61.5 216.0 %all-reduce.17.cloned.1.call-start = ((), (), s32[]{:S(2)}) async-start(), calls=%async_computation.3 | async-start | bytes 4194304 | tf_op jit(solution)/shard_map/psum | solution.py:67
  98.7 8.5 copy-start.19
  216.2 105.3 %all-reduce.29.cloned.1.call-start = ((), (), s32[]{:S(2)}) async-start(), calls=%async_computation.9 | async-start | bytes 262144 | tf_op jit(solution)/shard_map/psum | solution.py:52
  287.3 71.8 %all-reduce.19.cloned.1.call-start = ((), (), s32[]{:S(2)}) async-start(), calls=%async_computation.4 | async-start | bytes 393216 | tf_op jit(solution)/shard_map/psum | solution.py:52
  301.8 237.5 %all-reduce.21.cloned.1.call-start = ((), (), s32[]{:S(2)}) async-start(), calls=%async_computation.5 | async-start | bytes 4194304 | tf_op jit(solution)/shard_map/psum | solution.py:67
  342.2 19.4 %copy-start.24 = (f32[64,64]{1,0:T(8,128)S(1)}, f32[64,64]{1,0:T(8,128)}, u32[]{:S(2)}) copy-start(f32[64,64]{1,0:T(8,128)} %get-tuple-element.14) | copy-start | bytes 49156
  342.2 19.4 %copy-start.25 = (f32[64,64]{1,0:T(8,128)S(1)}, f32[64,64]{1,0:T(8,128)}, u32[]{:S(2)}) copy-start(f32[64,64]{1,0:T(8,128)} %get-tuple-element.15) | copy-start | bytes 49156
  344.3 26.2 %copy-start.7 = (f32[8192,64]{0,1:T(8,128)}, f32[8192,64]{0,1:T(8,128)S(1)}, u32[]{:S(2)}) copy-start(f32[8192,64]{0,1:T(8,128)S(1)} %convolution_subtract_fusion.1) | copy-start | bytes 6291460
  370.5 8.7 %copy-start.13 = (f32[64,8192]{1,0:T(8,128)S(1)}, f32[64,8192]{1,0:T(8,128)}, u32[]{:S(2)}) copy-start(f32[64,8192]{1,0:T(8,128)} %fusion.16) | copy-start | bytes 6291460
  381.5 96.4 %copy-start.5 = (f32[8192,64]{0,1:T(8,128)}, f32[8192,64]{0,1:T(8,128)S(1)}, u32[]{:S(2)}) copy-start(f32[8192,64]{0,1:T(8,128)S(1)} %convolution_add_fusion.2) | copy-start | bytes 6291460
  477.5 106.1 %all-reduce.27.cloned.1.call-start = ((), (), s32[]{:S(2)}) async-start(), calls=%async_computation.8 | async-start | bytes 262144 | tf_op jit(solution)/shard_map/psum | solution.py:52
  549.5 72.0 %all-reduce.23.cloned.1.call-start = ((), (), s32[]{:S(2)}) async-start(), calls=%async_computation.6 | async-start | bytes 393216 | tf_op jit(solution)/shard_map/psum | solution.py:52
  564.0 236.7 %all-reduce.25.cloned.1.call-start = ((), (), s32[]{:S(2)}) async-start(), calls=%async_computation.7 | async-start | bytes 4194304 | tf_op jit(solution)/shard_map/psum | solution.py:67
  604.4 19.7 %copy-start.22 = (f32[64,64]{1,0:T(8,128)S(1)}, f32[64,64]{1,0:T(8,128)}, u32[]{:S(2)}) copy-start(f32[64,64]{1,0:T(8,128)} %get-tuple-element.10) | copy-start | bytes 49156
  604.4 19.7 %copy-start.23 = (f32[64,64]{1,0:T(8,128)S(1)}, f32[64,64]{1,0:T(8,128)}, u32[]{:S(2)}) copy-start(f32[64,64]{1,0:T(8,128)} %get-tuple-element.11) | copy-start | bytes 49156
  606.5 26.5 %copy-start.10 = (f32[8192,64]{0,1:T(8,128)}, f32[8192,64]{0,1:T(8,128)S(1)}, u32[]{:S(2)}) copy-start(f32[8192,64]{0,1:T(8,128)S(1)} %convolution_subtract_fusion) | copy-start | bytes 6291460
  632.9 8.6 %copy-start.14 = (f32[64,8192]{1,0:T(8,128)S(1)}, f32[64,8192]{1,0:T(8,128)}, u32[]{:S(2)}) copy-start(f32[64,8192]{1,0:T(8,128)} %fusion.12) | copy-start | bytes 6291460
  739.9 5.0 copy-start.15
  840.4 4.1 copy-start.18
  (15 other events, 31.6 us)
Sparse Core Ops, SparseCore 0:
  9.5 13.2 all-gather.2
  24.4 25.8 all-gather.4
  61.6 36.1 all-reduce.14
  216.3 61.1 all-reduce.16
  287.4 33.9 all-reduce.28
  324.2 34.8 all-reduce.18
  477.6 61.6 all-reduce.20
  549.6 33.9 all-reduce.26
  586.5 34.9 all-reduce.22
  739.3 61.3 all-reduce.24
where the time goes:
time: 862 us; the launch traced here: 853 us
  matrix products  328 us (38%)
  waiting for transfers between devices  310 us (36%)
  blocking collectives  147 us (17%)
  other arithmetic  47.9 us (6%)
  between operations  15.6 us (2%)
    psum x3, waiting for transfers between devices, shards(): summed = lax.psum(feature_term, ('samples', 'rhs'))  165 us
    psum x3, blocking collectives, shards(): lax.psum(apply_partial_value, 'features').astype(jnp.bfloat16)  127 us
    psum x5, waiting for transfers between devices, totals(): return lax.psum(values, 'features')  105 us
    dot_general x3, matrix products, shards(): jnp.dot(design, narrow, preferred_element_type=jnp.float32)  85.3 us
    dot_general x3, matrix products, shards(): lax.dot_general(design, narrow_images, (((0,), (0,)), ((), ())), preferre...  77.8 us
    dot_general x12, matrix products, inner_prod(): lax.dot_general(left, right, (((0,), (0,)), ((), ())), precision=lax.Prec...  30.3 us
    dot_general x3, matrix products, factor_times(): second = jnp.dot(factor_narrow, lower, preferred_element_type=jnp.float32)  27.1 us
    all_gather x1, waiting for transfers between devices, shards(): basis_rows = lax.all_gather(factor, 'rhs', axis=1, tiled=True)  25.6 us
  transfers between devices with their start and end apart: 10, of which 10 were waited for; matrix products, arithmetic and copies ran while one was open for 11% of the time, Pallas kernels for 0%

commit v1 on v0

v1 whole, which is shorter than its diff:
```python
import functools

import jax
import jax.numpy as jnp
from jax import lax
from jax.experimental import pallas as pl
from jax.experimental.pallas import tpu as pltpu
from jax.sharding import PartitionSpec as P

ITERS = 3
MESH = pl.DeviceIdType.MESH
RIDGE = 1.0


def dot_t(left, right):
    return lax.dot_general(
        left,
        right,
        (((1,), (1,)), ((), ())),
        precision=lax.Precision.HIGHEST,
        preferred_element_type=jnp.float32,
    )


def dot_h(left, right):
    return jnp.dot(
        left, right, precision=lax.Precision.HIGHEST, preferred_element_type=jnp.float32
    )


def feature_group(n_rhs):
    me = lax.axis_index("samples") * n_rhs + lax.axis_index("rhs")

    def place(index):
        return {"samples": lax.div(index, n_rhs), "rhs": lax.rem(index, n_rhs)}

    return me, place


def sample_group():
    return lax.axis_index("features"), lambda index: {"features": index}


def others(n, me, body):
    for step in range(1, n):
        body(lax.rem(me + step, n))


def greet(groups):
    barrier = pltpu.get_barrier_semaphore()
    total = 0
    for n, me, place in groups:
        others(
            n,
            me,
            lambda peer: pl.semaphore_signal(
                barrier, inc=1, device_id=place(peer), device_id_type=MESH
            ),
        )
        total += n - 1
    pl.semaphore_wait(barrier, total)


def columns(index, width):
    return pl.ds(pl.multiple_of(index * width, 128), width)


def exchange(n, me, place, source, target, send_sem, recv_sem):
    def copy(step):
        peer = lax.rem(me + step, n)
        return pltpu.make_async_remote_copy(
            src_ref=source(peer),
            dst_ref=target(me),
            send_sem=send_sem.at[step],
            recv_sem=recv_sem.at[step],
            device_id=place(peer),
            device_id_type=MESH,
        )

    copies = [copy(step) for step in range(1, n)]
    for each in copies:
        each.start()
    for each in copies:
        each.wait_recv()
    return copies


def finish(copies):
    for each in copies:
        each.wait_send()


def total_of(own, held, n, me):
    total = own.astype(jnp.float32)
    for step in range(1, n):
        total = total + held[lax.rem(me + step, n)].astype(jnp.float32)
    return total


def images_kernel(n, x_ref, out_ref, held, send_a, recv_a, send_b, recv_b):
    me, place = sample_group()
    width = x_ref.shape[1] // n
    greet([(n, me, place)])
    first = exchange(
        n, me, place,
        lambda peer: x_ref.at[:, columns(peer, width)],
        lambda index: held.at[index],
        send_a, recv_a,
    )
    own = x_ref[:, columns(me, width)]
    out_ref[:, columns(me, width)] = total_of(own, held, n, me).astype(out_ref.dtype)
    second = exchange(
        n, me, place,
        lambda peer: out_ref.at[:, columns(me, width)],
        lambda index: out_ref.at[:, columns(index, width)],
        send_b, recv_b,
    )
    finish(first + second)


def scatter_kernel(n, n_rhs, x_ref, out_ref, held, send_a, recv_a):
    me, place = feature_group(n_rhs)
    width = x_ref.shape[1] // n
    greet([(n, me, place)])
    first = exchange(
        n, me, place,
        lambda peer: x_ref.at[:, columns(peer, width)],
        lambda index: held.at[index],
        send_a, recv_a,
    )
    out_ref[...] = total_of(x_ref[:, columns(me, width)], held, n, me)
    finish(first)


def gather_kernel(n, n_rhs, split, x_ref, out_ref, send_a, recv_a):
    me, place = feature_group(n_rhs)
    rows, wide = out_ref.shape
    width = wide // n

    def part(peer):
        if split:
            return pl.ds(pl.multiple_of(lax.rem(peer, n_rhs) * rows, 16), rows)
        return pl.ds(0, rows)

    greet([(n, me, place)])
    first = exchange(
        n, me, place,
        lambda peer: x_ref.at[part(peer), :],
        lambda index: out_ref.at[:, columns(index, width)],
        send_a, recv_a,
    )
    out_ref[:, columns(me, width)] = x_ref[part(me), :]
    finish(first)


def totals_kernel(
    n, n_rhs, n_feat, x_ref, out_ref, held, across, mine, sa, ra, sb, rb, sc, rc
):
    me, place = feature_group(n_rhs)
    feat, feat_place = sample_group()
    width = x_ref.shape[1] // n
    greet([(n, me, place), (n_feat, feat, feat_place)])
    first = exchange(
        n, me, place,
        lambda peer: x_ref.at[:, columns(peer, width)],
        lambda index: held.at[index],
        sa, ra,
    )
    mine[...] = total_of(x_ref[:, columns(me, width)], held, n, me)
    second = exchange(
        n_feat, feat, feat_place,
        lambda peer: mine,
        lambda index: across.at[index],
        sb, rb,
    )
    across[feat] = mine[...]
    total = across[0]
    for index in range(1, n_feat):
        total = total + across[index]
    out_ref[:, columns(me, width)] = total
    third = exchange(
        n, me, place,
        lambda peer: out_ref.at[:, columns(me, width)],
        lambda index: out_ref.at[:, columns(index, width)],
        sc, rc,
    )
    finish(first + second + third)


def call(kernel, name, ident, shape, dtype, scratch, sems, *args):
    return pl.pallas_call(
        kernel,
        name=name,
        out_shape=jax.ShapeDtypeStruct(shape, dtype),
        in_specs=[pl.BlockSpec(memory_space=pltpu.VMEM)] * len(args),
        out_specs=pl.BlockSpec(memory_space=pltpu.VMEM),
        scratch_shapes=[pltpu.VMEM(s, d) for s, d in scratch]
        + [pltpu.SemaphoreType.DMA((count,)) for count in sems],
        compiler_params=pltpu.CompilerParams(collective_id=ident, has_side_effects=True),
    )(*args)


def shards(n_samp, n_feat, n_rhs, design, right_side, factor, nystrom_values):
    feat_rows, col_share = right_side.shape
    samples = design.shape[0]
    width = col_share * n_rhs
    rank = nystrom_values.shape[0]
    n = n_samp * n_rhs
    piece = feat_rows // n
    samp, rhs = lax.axis_index("samples"), lax.axis_index("rhs")
    shrink = (1.0 + jnp.min(nystrom_values)) / (1.0 + nystrom_values) - 1.0

    def own_rows(block):
        def rows_for(core):
            return lax.dynamic_slice_in_dim(block, (samp * n_rhs + core) * piece, piece, 0)

        parts = [None] * n_rhs
        moved = [rows_for(rhs)]
        for step in range(1, n_rhs):
            pairs = [(i, (i + step) % n_rhs) for i in range(n_rhs)]
            moved.append(lax.ppermute(rows_for((rhs + step) % n_rhs), "rhs", pairs))
        for core in range(n_rhs):
            best = moved[0]
            for step in range(1, n_rhs):
                best = jnp.where((rhs - step) % n_rhs == core, moved[step], best)
            parts[core] = best
        return jnp.concatenate(parts, axis=1)

    images_of = lambda x: call(
        functools.partial(images_kernel, n_feat), "images_sum", 1, x.shape, jnp.bfloat16,
        [((n_feat, width, samples // n_feat), jnp.bfloat16)], [n_feat] * 4, x,
    )
    scatter = lambda x: call(
        functools.partial(scatter_kernel, n, n_rhs), "feature_scatter", 2,
        (width, piece), jnp.float32, [((n, width, piece), jnp.bfloat16)], [n] * 2, x,
    )
    gather = lambda x: call(
        functools.partial(gather_kernel, n, n_rhs, False), "direction_gather", 3,
        (width, feat_rows), x.dtype, [], [n] * 2, x,
    )
    gather_out = lambda x: call(
        functools.partial(gather_kernel, n, n_rhs, True), "output_gather", 4,
        (x.shape[0] // n_rhs, feat_rows), x.dtype, [], [n] * 2, x,
    )

    def totals(x):
        lanes = x.shape[1]
        unit = 128 * n
        padded = -(-lanes // unit) * unit
        x = jnp.pad(x, ((0, 0), (0, padded - lanes)))
        share = (width, padded // n)
        got = call(
            functools.partial(totals_kernel, n, n_rhs, n_feat), "small_totals", 5,
            x.shape, jnp.float32,
            [((n,) + share, jnp.float32), ((n_feat,) + share, jnp.float32), (share, jnp.float32)],
            [n, n, n_feat, n_feat, n, n], x,
        )
        return got[:, :lanes]

    basis = own_rows(factor)
    residual = own_rows(right_side).T

    def parts_of(values):
        upper = values.astype(jnp.bfloat16)
        widened = lax.optimization_barrier(upper).astype(jnp.float32)
        return jnp.concatenate([upper, (values - widened).astype(jnp.bfloat16)], axis=0)

    def factor_inner(values):
        both = jnp.dot(parts_of(values), basis, preferred_element_type=jnp.float32)
        return both[:width] + both[width:]

    def expand(projected):
        both = lax.dot_general(
            parts_of(shrink[None, :] * projected), basis, (((1,), (1,)), ((), ())),
            preferred_element_type=jnp.float32,
        )
        return both[:width] + both[width:]

    projected = totals(factor_inner(residual))
    direction = residual + expand(projected)
    solution = jnp.zeros_like(residual)
    eye = jnp.eye(width, dtype=jnp.float32)
    for iteration in range(ITERS):
        narrow = gather(direction.astype(jnp.bfloat16))
        partial = lax.dot_general(
            narrow, design, (((1,), (1,)), ((), ())), preferred_element_type=jnp.float32
        )
        images = images_of(partial.astype(jnp.bfloat16))
        feature_term = jnp.dot(images, design, preferred_element_type=jnp.float32)
        applied = scatter(feature_term.astype(jnp.bfloat16)) + RIDGE * direction
        last = iteration + 1 == ITERS
        block = dot_t(
            jnp.concatenate([direction, applied], axis=0),
            jnp.concatenate([applied, residual], axis=0),
        )
        small = [block[:width], block[width:]]
        if not last:
            small.append(factor_inner(applied))
        summed = totals(jnp.concatenate(small, axis=1))
        gram = summed[:, :width]
        cross = summed[:, width : 2 * width]
        gram = 0.5 * (gram + gram.T)
        chol_lower = jnp.linalg.cholesky(gram)
        inverse = jax.scipy.linalg.solve_triangular(chol_lower, eye, lower=True)
        back_t = dot_h(dot_h(inverse, cross).T, inverse)
        solution = solution + dot_h(back_t, direction)
        residual = residual - dot_h(back_t, applied)
        if not last:
            image_image = summed[:, 2 * width : 3 * width]
            image_res = summed[:, 3 * width : 4 * width]
            factor_image = summed[:, 4 * width :]
            projected = projected - dot_h(back_t, factor_image)
            scaled = residual + expand(projected)
            image_new = image_res - dot_t(image_image, back_t)
            image_new = image_new + dot_t(factor_image, shrink[None, :] * projected)
            next_t = dot_h(dot_h(inverse, image_new).T, inverse)
            direction = scaled - dot_h(next_t, direction)
    stacked = []
    for core in range(n_rhs):
        rows = slice(core * col_share, (core + 1) * col_share)
        stacked += [solution[rows], residual[rows]]
    whole = gather_out(jnp.concatenate(stacked, axis=0).astype(jnp.bfloat16))
    whole = whole.astype(jnp.float32)
    return whole[:col_share].T, whole[col_share:].T


def solution(mesh):
    placed = (P(("samples", "rhs"), "features"), P("features", "rhs"), P("features", "rhs"), P())
    sizes = (mesh.shape["samples"], mesh.shape["features"], mesh.shape["rhs"])
    return jax.shard_map(
        functools.partial(shards, *sizes),
        mesh=mesh,
        in_specs=placed,
        out_specs=(P("features", "rhs"), P("features", "rhs")),
        check_vma=False,
    )
```

time: 862 us -> 523 us (0.61)
  waiting for transfers between devices: 310 us -> 0.01 us
  Pallas kernels: 0 us -> 274 us
  blocking collectives: 147 us -> 0 us
  matrix products: 328 us -> 183 us
  between operations: 15.6 us -> 1.91 us
    pallas_call x0 -> x14, Pallas kernels: none -> 274 us  [call(): pl.pallas_call(kernel, name=name, out_shape=jax.ShapeDtypeStruct(shape, d...]
    psum x8 -> x0, waiting for transfers between devices: 270 us -> none  [the longest x3 165 us: shards(): summed = lax.psum(feature_term, ('samples', 'rhs'))]
    psum x4 -> x0, blocking collectives: 147 us -> none  [the longest x3 127 us: shards(): lax.psum(apply_partial_value, 'features').astype(jnp.bfloat16)]
    dot_general x42 -> x39, matrix products: 309 us -> 182 us  [the longest x3 85.1 us: shards(): lax.dot_general(narrow, design, (((1,), (1,)), ((), ())), preferred_eleme...]
    all_gather x2 -> x0, waiting for transfers between devices: 38.5 us -> none  [the longest x1 25.6 us: shards(): basis_rows = lax.all_gather(factor, 'rhs', axis=1, tiled=True)]
    another operation x13 -> x3, matrix products: 18.9 us -> 0.76 us  [shards(): inverse = jax.scipy.linalg.solve_triangular(chol_lower, eye, lower=True)]
  transfers between devices with their start and end apart: 10 -> 2, of which waited for: 10 -> 0; matrix products, arithmetic and copies ran while one was open for 11% -> 1% of each run, Pallas kernels for 0% -> 0%
where the time goes in v1:
time: 523 us; the launch traced here: 520 us
  Pallas kernels  274 us (52%)
  matrix products  183 us (35%)
  other arithmetic  53.2 us (10%)
  local copies, waits for them, and re-layouts  7.11 us (1%)
    pallas_call x14, Pallas kernels, call(): pl.pallas_call(kernel, name=name, out_shape=jax.ShapeDtypeStruct(shape, d...  274 us
    dot_general x3, matrix products, shards(): lax.dot_general(narrow, design, (((1,), (1,)), ((), ())), preferred_eleme...  85.1 us
    dot_general x3, matrix products, shards(): feature_term = jnp.dot(images, design, preferred_element_type=jnp.float32)  76.7 us
    another operation x9, other arithmetic, shards(): chol_lower = jnp.linalg.cholesky(gram)  19.6 us
    another operation x6, other arithmetic, shards(): inverse = jax.scipy.linalg.solve_triangular(chol_lower, eye, lower=True)  16.6 us
    dot_general x20, matrix products, dot_h(): jnp.dot(left, right, precision=lax.Precision.HIGHEST, preferred_element_t...  11.2 us
  transfers between devices with their start and end apart: 2, of which 0 were waited for; matrix products, arithmetic and copies ran while one was open for 1% of the time, Pallas kernels for 0%

profile of v1, /device:TPU:0, one launch (start us, length us, event | category | flops | bytes accessed | tf_op | source)
XLA Modules:
  0.0 520.3 jit_solution(17878659787915153946)
XLA Ops:
  9.9 20.1 %small_totals.4 = f32[64,1024]{1,0:T(8,128)} custom-call(f32[64,1024]{1,0:T(8,128)} %pad.8.x_ref), custom_call_target="tpu_custom_call" | custom-call | tf_op jit(solution)/shard_map/small_totals/pallas_call | solution.py:191
  33.3 15.2 %direction_gather.3 = bf16[64,8192]{1,0:T(8,128)(2,1)} custom-call(bf16[64,1024]{1,0:T(8,128)(2,1)} %get-tuple-element.8.x_ref), custom_call_target="tpu_custom_call" | custom-call | tf_op jit(solution)/shard_map/direction_gather/pallas_call | solution.py:191
  48.5 28.2 %convolution_convert_fusion.5.x_ref = bf16[64,4096]{1,0:T(8,128)(2,1)} fusion(bf16[64,8192]{1,0:T(8,128)(2,1)} %direction_gather.3, bf16[4096,8192]{1,0:T(8,128)(2,1)} %param.7), kind=kOutput, calls=%fused_computation.5 | convolution fusion | flops 4295229440 | bytes 68681728 | tf_op jit(solution)/shard_map/dot_general | solution.py:285
  76.8 26.8 %images_sum.3 = bf16[64,4096]{1,0:T(8,128)(2,1)} custom-call(bf16[64,4096]{1,0:T(8,128)(2,1)} %convolution_convert_fusion.5.x_ref), custom_call_target="tpu_custom_call" | custom-call | tf_op jit(solution)/shard_map/images_sum/pallas_call | solution.py:191
  103.6 25.6 %convolution_convert_fusion.2.x_ref = bf16[64,8192]{1,0:T(8,128)(2,1)} fusion(bf16[64,4096]{1,0:T(8,128)(2,1)} %images_sum.3, bf16[4096,8192]{1,0:T(8,128)(2,1)} %param.7), kind=kOutput, calls=%fused_computation.2 | convolution fusion | flops 4295491584 | bytes 68681728 | tf_op jit(solution)/shard_map/dot_general | solution.py:289
  129.1 15.1 %feature_scatter.3 = f32[64,1024]{1,0:T(8,128)} custom-call(bf16[64,8192]{1,0:T(8,128)(2,1)} %convolution_convert_fusion.2.x_ref), custom_call_target="tpu_custom_call" | custom-call | tf_op jit(solution)/shard_map/feature_scatter/pallas_call | solution.py:191
  147.0 22.3 %small_totals.5 = f32[64,1024]{1,0:T(8,128)} custom-call(f32[64,1024]{1,0:T(8,128)} %pad_maximum_fusion.1.x_ref), custom_call_target="tpu_custom_call" | custom-call | tf_op jit(solution)/shard_map/small_totals/pallas_call | solution.py:191
  171.0 5.8 %cholesky.59 = f32[64,64]{1,0:T(8,128)S(1)} custom-call(f32[64,64]{1,0:T(8,128)S(1)} %fusion.77), custom_call_target="Cholesky" | custom-call | tf_op jit(solution)/shard_map/jit(cholesky)/cholesky | solution.py:303
  190.6 15.4 %direction_gather.4 = bf16[64,8192]{1,0:T(8,128)(2,1)} custom-call(bf16[64,1024]{1,0:T(8,128)(2,1)} %get-tuple-element.28.x_ref), custom_call_target="tpu_custom_call" | custom-call | tf_op jit(solution)/shard_map/direction_gather/pallas_call | solution.py:191
  206.0 28.4 %convolution_convert_fusion.4.x_ref = bf16[64,4096]{1,0:T(8,128)(2,1)} fusion(bf16[64,8192]{1,0:T(8,128)(2,1)} %direction_gather.4, bf16[4096,8192]{1,0:T(8,128)(2,1)} %param.7), kind=kOutput, calls=%fused_computation.4 | convolution fusion | flops 4295229440 | bytes 68681728 | tf_op jit(solution)/shard_map/dot_general | solution.py:285
  234.4 26.8 %images_sum.4 = bf16[64,4096]{1,0:T(8,128)(2,1)} custom-call(bf16[64,4096]{1,0:T(8,128)(2,1)} %convolution_convert_fusion.4.x_ref), custom_call_target="tpu_custom_call" | custom-call | tf_op jit(solution)/shard_map/images_sum/pallas_call | solution.py:191
  261.2 25.6 %convolution_convert_fusion.1.x_ref = bf16[64,8192]{1,0:T(8,128)(2,1)} fusion(bf16[64,4096]{1,0:T(8,128)(2,1)} %images_sum.4, bf16[4096,8192]{1,0:T(8,128)(2,1)} %param.7), kind=kOutput, calls=%fused_computation.1 | convolution fusion | flops 4295491584 | bytes 68681728 | tf_op jit(solution)/shard_map/dot_general | solution.py:289
  286.7 15.0 %feature_scatter.4 = f32[64,1024]{1,0:T(8,128)} custom-call(bf16[64,8192]{1,0:T(8,128)(2,1)} %convolution_convert_fusion.1.x_ref), custom_call_target="tpu_custom_call" | custom-call | tf_op jit(solution)/shard_map/feature_scatter/pallas_call | solution.py:191
  304.5 22.2 %small_totals.6 = f32[64,1024]{1,0:T(8,128)} custom-call(f32[64,1024]{1,0:T(8,128)} %pad_maximum_fusion.2.x_ref), custom_call_target="tpu_custom_call" | custom-call | tf_op jit(solution)/shard_map/small_totals/pallas_call | solution.py:191
  328.4 5.8 %cholesky.70 = f32[64,64]{1,0:T(8,128)S(1)} custom-call(f32[64,64]{1,0:T(8,128)S(1)} %fusion.74), custom_call_target="Cholesky" | custom-call | tf_op jit(solution)/shard_map/jit(cholesky)/cholesky | solution.py:303
  348.4 15.3 %direction_gather.5 = bf16[64,8192]{1,0:T(8,128)(2,1)} custom-call(bf16[64,1024]{1,0:T(8,128)(2,1)} %get-tuple-element.32.x_ref), custom_call_target="tpu_custom_call" | custom-call | tf_op jit(solution)/shard_map/direction_gather/pallas_call | solution.py:191
  363.7 28.5 %convolution_convert_fusion.3.x_ref = bf16[64,4096]{1,0:T(8,128)(2,1)} fusion(bf16[64,8192]{1,0:T(8,128)(2,1)} %direction_gather.5, bf16[4096,8192]{1,0:T(8,128)(2,1)} %param.7), kind=kOutput, calls=%fused_computation.3 | convolution fusion | flops 4295229440 | bytes 68681728 | tf_op jit(solution)/shard_map/dot_general | solution.py:285
  392.2 26.7 %images_sum.5 = bf16[64,4096]{1,0:T(8,128)(2,1)} custom-call(bf16[64,4096]{1,0:T(8,128)(2,1)} %convolution_convert_fusion.3.x_ref), custom_call_target="tpu_custom_call" | custom-call | tf_op jit(solution)/shard_map/images_sum/pallas_call | solution.py:191
  418.9 25.6 %convolution_convert_fusion.x_ref = bf16[64,8192]{1,0:T(8,128)(2,1)} fusion(bf16[64,4096]{1,0:T(8,128)(2,1)} %images_sum.5, bf16[4096,8192]{1,0:T(8,128)(2,1)} %param.7), kind=kOutput, calls=%fused_computation | convolution fusion | flops 4295491584 | bytes 68681728 | tf_op jit(solution)/shard_map/dot_general | solution.py:289
  444.5 15.3 %feature_scatter.5 = f32[64,1024]{1,0:T(8,128)} custom-call(bf16[64,8192]{1,0:T(8,128)(2,1)} %convolution_convert_fusion.x_ref), custom_call_target="tpu_custom_call" | custom-call | tf_op jit(solution)/shard_map/feature_scatter/pallas_call | solution.py:191
  462.1 22.8 %small_totals.7 = f32[64,1024]{1,0:T(8,128)} custom-call(f32[64,1024]{1,0:T(8,128)} %select_maximum_fusion.x_ref), custom_call_target="tpu_custom_call" | custom-call | tf_op jit(solution)/shard_map/small_totals/pallas_call | solution.py:191
  486.6 5.8 %cholesky.81 = f32[64,64]{1,0:T(8,128)S(1)} custom-call(f32[64,64]{1,0:T(8,128)S(1)} %fusion.71), custom_call_target="Cholesky" | custom-call | tf_op jit(solution)/shard_map/jit(cholesky)/cholesky | solution.py:303
  493.8 4.9 custom-call.9
  502.0 15.4 %output_gather.1 = bf16[64,8192]{1,0:T(8,128)(2,1)} custom-call(bf16[128,1024]{1,0:T(8,128)(2,1)} %pad_maximum_fusion.3.x_ref), custom_call_target="tpu_custom_call" | custom-call | tf_op jit(solution)/shard_map/output_gather/pallas_call | solution.py:191
  (101 shorter events, 59.8 us)
Async XLA Ops:
  1.9 5.2 %collective-permute-start.1 = (bf16[1024,384]{1,0:T(8,128)(2,1)S(1)}, bf16[1024,384]{1,0:T(8,128)(2,1)}, u32[]{:S(2)}, u32[]{:S(2)}) collective-permute-start(bf16[1024,384]{1,0:T(8,128)(2,1)S(1)} %constant_dynamic-slice_fusion), channel_id=1, source_target_pairs={{0,1},{1,0},{2,3},{3,2},{4,5},{5,4},{6,7},{7,6},{8,9},{9,8},{10,11... | collective-permute-start | bytes 2359304 | tf_op jit(solution)/shard_map/ppermute | solution.py:221
  3.3 2.7 collective-permute-start
  145.8 38.7 %copy-start = (f32[64,1024]{1,0:T(8,128)S(1)}, f32[64,1024]{1,0:T(8,128)}, u32[]{:S(2)}) copy-start(f32[64,1024]{1,0:T(8,128)} %small_totals.4) | copy-start | bytes 786436
